TPU v7x, 256 devices: a whole 4x4x8 slice. The times are simulated.
256 devices in a mesh: batch: 4 (over x), proto: 64 (over y, z, core).
Axes of the slice: x: 4, y: 4, z: 8, core: 2. Of those that a mesh axis runs over, the one named last changes fastest.
Arguments:
- view_codes: bfloat16 [4096, 1024], P('batch', 'proto'), may hold values from -80 to 80
- predictor_view_embeddings: bfloat16 [4096, 1024], P('batch', 'proto'), may hold values from -80 to 80
- prototypes: bfloat16 [65536, 1024], P('proto'), may hold values from -64 to 64
Outputs:
- assignments: bfloat16 [4096, 65536], P('batch', 'proto')
- loss_rows: float32 [4096], P('batch')
All inputs are finite; a program needn't handle non-finite values.
Results may differ from a plain program's by a relative error of at most 0.0034.
Values may be sent and summed in bfloat16 or wider, within the bound.
A program may use at most 64 MiB of HBM per device.

v0:
```python
import jax
import jax.numpy as jnp
from jax import lax
from jax.sharding import PartitionSpec as P

SINK_ITERS = 3
EPSILON = 0.05
SOFTMAX_TEMP_VALUE = 0.1


def copy_for_each(shard, axis):
    copies = jnp.broadcast_to(shard, (lax.axis_size(axis), *shard.shape))
    return lax.all_to_all(copies, axis, split_axis=0, concat_axis=0, tiled=True)


def of_everyone(shard, axis):
    return copy_for_each(shard, axis).sum(axis=0)


def together(arrays, axis):
    ravelled, at, gathered = (jnp.concatenate([a.reshape(-1) for a in arrays]), 0, [])
    subtotal = of_everyone(ravelled, axis)
    for a in arrays:
        gathered.append(subtotal[at : at + a.size].reshape(a.shape))
        at += a.size
    return tuple(gathered)


def normalized(prototypes):
    weights = prototypes.astype(jnp.float32)
    return (weights * lax.rsqrt(jnp.sum(weights * weights, axis=1, keepdims=True) + 1e-06)).astype(
        jnp.bfloat16
    )


def view_scores(embedded, unit_prototype_rows):
    products = jnp.dot(embedded, unit_prototype_rows.T, preferred_element_type=jnp.float32)
    values = embedded.astype(jnp.float32)
    inverse_factor = lax.rsqrt(jnp.sum(values * values, axis=1) + 1e-06)
    return products * inverse_factor[:, None]


def local(view_codes, predictor_view_embeddings, prototypes):
    unit_prototype_rows = normalized(prototypes)
    whole_first, whole_second = (
        lax.all_gather(view_codes, "proto", axis=1, tiled=True),
        lax.all_gather(predictor_view_embeddings, "proto", axis=1, tiled=True),
    )
    scores_codes = view_scores(whole_first, unit_prototype_rows)
    predictor_scores = view_scores(whole_second, unit_prototype_rows)
    kernel = jnp.exp(scores_codes / EPSILON)
    rows_total = kernel.shape[0] * lax.axis_size("batch")
    protos_total = kernel.shape[1] * lax.axis_size("proto")
    logit_scores = predictor_scores / SOFTMAX_TEMP_VALUE
    scale_rows = jnp.ones((kernel.shape[0],), jnp.float32)
    for iteration in range(SINK_ITERS):
        col_part = jnp.dot(scale_rows, kernel, precision=lax.Precision.HIGHEST)
        col_sums = of_everyone(col_part, "batch")
        scale_cols = 1.0 / (protos_total * col_sums)
        row_part = jnp.dot(kernel, scale_cols, precision=lax.Precision.HIGHEST)
        row_sums = of_everyone(row_part, "proto")
        scale_rows = 1.0 / (rows_total * row_sums)
    assign = kernel * scale_cols[None, :] * (rows_total * scale_rows)[:, None]
    assignments = (protos_total * assign).astype(jnp.bfloat16)
    cross_part = jnp.sum(assign * logit_scores, axis=1)
    totals, cross_term = together((jnp.sum(jnp.exp(logit_scores), axis=1), cross_part), "proto")
    loss_rows = jnp.log(totals) - cross_term
    return (assignments, loss_rows)


def solution(mesh):
    placed = (P("batch", "proto"), P("batch", "proto"), P("proto", None))
    return jax.shard_map(
        local,
        mesh=mesh,
        in_specs=placed,
        out_specs=(P("batch", "proto"), P("batch")),
        check_vma=False,
    )
```

profile of v0, /device:TPU:1, one launch (start us, length us, event | category | flops | bytes accessed | tf_op | source)
XLA Modules:
  0.0 249.5 jit_solution(1705991306893637967)
XLA Ops:
  7.2 0.0 copy-start.1
  7.2 0.0 all-gather.3.cloned.1.call-start
  7.2 0.7 all-gather.3.cloned.1.call-update
  7.9 0.0 all-gather.5.cloned.1.call-start
  8.0 0.7 all-gather.5.cloned.1.call-update
  8.7 2.1 fusion
  10.7 81.8 %all-gather.3.cloned.1.call-done = bf16[1024,1024]{0,1:T(8,128)(2,1)} async-done(((bf16[1024,16]{0,1:T(8,128)(2,1)}), bf16[1024,1024]{0,1:T(8,128)(2,1)}) %all-gather.3.cloned.1.call-update) | async-done | bytes 2097168 | tf_op jit(solution)/shard_map/all_gather | solution.py:46
  92.6 2.1 multiply_reduce_fusion.1
  94.6 0.0 copy-done.1
  94.7 4.0 %multiply_exponential_fusion = f32[1024,1024]{1,0:T(8,128)S(1)} fusion(bf16[1024,1024]{0,1:T(8,128)(2,1)} %all-gather.3.cloned.1.call-done, f32[1024]{0:T(1024)S(1)} %add_rsqrt_fusion.1, bf16[1024,1024]{1,0:T(8,128)(2,1)S(1)} %copy-done.1, f32[1024]{0:T(1024)S(1)} %add_rsqrt_fusion.2), kind=kOutput, calls=%fused_computation.25 | convolution fusion | flops 2152726528 | bytes 8396800 | tf_op jit(solution)/shard_map/dot_general | solution.py:37
  98.6 0.0 copy-start
  98.7 1.9 copy-done
  100.6 3.6 %fusion.14 = f32[1,1024]{1,0:T(1,128)S(1)} fusion(f32[1024,1024]{1,0:T(8,128)S(1)} %multiply_exponential_fusion), kind=kOutput, calls=%fused_computation.19 | convolution fusion | flops 12582912 | bytes 4198400 | tf_op jit(solution)/shard_map/dot_general | solution.py:57
  104.2 8.1 %all_to_all.42 = f32[4,1,1024]{2,1,0:T(1,128)S(1)} all-to-all(f32[4,1,1024]{2,1,0:T(1,128)S(1)} %broadcast_in_dim.26), channel_id=1, replica_groups=mesh['batch'=4,'proto'=64] {'batch'}, dimensions={0} | all-to-all | bytes 32768 | tf_op jit(solution)/shard_map/all_to_all | solution.py:13
  112.2 4.4 %fusion.12 = f32[1,1024]{1,0:T(1,128)S(1)} fusion(f32[1024,1]{0,1:T(1,128)S(1)} %bitcast.52, f32[1024,1024]{1,0:T(8,128)} %copy-done), kind=kOutput, calls=%fused_computation.17 | convolution fusion | flops 12582912 | bytes 4202496 | tf_op jit(solution)/shard_map/dot_general | solution.py:60
  116.7 0.1 broadcast_in_dim.27
  116.8 19.7 %all_to_all.43 = f32[64,1,1024]{2,1,0:T(1,128)S(1)} all-to-all(f32[64,1,1024]{2,1,0:T(1,128)S(1)} %broadcast_in_dim.27), channel_id=1, replica_groups=mesh['batch'=4,'proto'=64] {'proto'}, dimensions={0} | all-to-all | bytes 524288 | tf_op jit(solution)/shard_map/all_to_all | solution.py:13
  136.5 0.2 reduce_sum.111
  136.7 5.6 %fusion.10 = f32[1,1024]{1,0:T(1,128)S(1)} fusion(f32[1024,1]{0,1:T(1,128)S(1)} %bitcast.53, f32[1024,1024]{1,0:T(8,128)} %copy-done), kind=kOutput, calls=%fused_computation.15 | convolution fusion | flops 12582912 | bytes 4202496 | tf_op jit(solution)/shard_map/dot_general | solution.py:57
  142.4 6.6 %all_to_all.44 = f32[4,1,1024]{2,1,0:T(1,128)S(1)} all-to-all(f32[4,1,1024]{2,1,0:T(1,128)S(1)} %broadcast_in_dim.28), channel_id=1, replica_groups=mesh['batch'=4,'proto'=64] {'batch'}, dimensions={0} | all-to-all | bytes 32768 | tf_op jit(solution)/shard_map/all_to_all | solution.py:13
  149.0 4.4 %fusion.8 = f32[1,1024]{1,0:T(1,128)S(1)} fusion(f32[1024,1]{0,1:T(1,128)S(1)} %bitcast.54, f32[1024,1024]{1,0:T(8,128)} %copy-done), kind=kOutput, calls=%fused_computation.13 | convolution fusion | flops 12582912 | bytes 4202496 | tf_op jit(solution)/shard_map/dot_general | solution.py:60
  153.4 0.1 broadcast_in_dim.29
  153.6 19.1 %all_to_all.45 = f32[64,1,1024]{2,1,0:T(1,128)S(1)} all-to-all(f32[64,1,1024]{2,1,0:T(1,128)S(1)} %broadcast_in_dim.29), channel_id=1, replica_groups=mesh['batch'=4,'proto'=64] {'proto'}, dimensions={0} | all-to-all | bytes 524288 | tf_op jit(solution)/shard_map/all_to_all | solution.py:13
  172.6 0.2 reduce_sum.113
  172.8 5.6 %fusion.6 = f32[1,1024]{1,0:T(1,128)S(1)} fusion(f32[1024,1]{0,1:T(1,128)S(1)} %bitcast.55, f32[1024,1024]{1,0:T(8,128)} %copy-done), kind=kOutput, calls=%fused_computation.11 | convolution fusion | flops 12582912 | bytes 4202496 | tf_op jit(solution)/shard_map/dot_general | solution.py:57
  178.5 6.6 %all_to_all.46 = f32[4,1,1024]{2,1,0:T(1,128)S(1)} all-to-all(f32[4,1,1024]{2,1,0:T(1,128)S(1)} %broadcast_in_dim.30), channel_id=1, replica_groups=mesh['batch'=4,'proto'=64] {'batch'}, dimensions={0} | all-to-all | bytes 32768 | tf_op jit(solution)/shard_map/all_to_all | solution.py:13
  185.1 4.4 %fusion.4 = f32[1,1024]{1,0:T(1,128)S(1)} fusion(f32[1024,1]{0,1:T(1,128)S(1)} %bitcast.51, f32[1024,1024]{1,0:T(8,128)} %copy-done), kind=kOutput, calls=%fused_computation.8 | convolution fusion | flops 12582912 | bytes 4202496 | tf_op jit(solution)/shard_map/dot_general | solution.py:60
  189.5 0.8 broadcast_in_dim.31
  190.4 7.9 %all-to-all-start.5 = ((f32[64,1,1024]{2,1,0:T(1,128)}), f32[64,1,1024]{2,1,0:T(1,128)S(1)}, u32[]{:S(2)}, u32[]{:S(2)}) async-start(f32[64,1,1024]{2,1,0:T(1,128)} %broadcast_in_dim.31), calls=%async_computation.5 | async-start | bytes 524288 | tf_op jit(solution)/shard_map/all_to_all | solution.py:13
  198.3 0.0 all-gather.5.cloned.1.call-done
  198.3 2.1 multiply_reduce_fusion
  200.4 9.9 %all-to-all-done.5 = f32[64,1,1024]{2,1,0:T(1,128)S(1)} async-done(((f32[64,1,1024]{2,1,0:T(1,128)}), f32[64,1,1024]{2,1,0:T(1,128)S(1)}, u32[]{:S(2)}, u32[]{:S(2)}) %all-to-all-start.5) | async-done | bytes 262176 | tf_op jit(solution)/shard_map/all_to_all | solution.py:13
  210.3 0.2 reduce_sum.115
  210.5 6.9 %fusion.2 = (f32[1024]{0:T(1024)S(1)}, f32[1024]{0:T(1024)S(1)}, bf16[1024,1024]{0,1:T(8,128)(2,1)}) fusion(f32[1024]{0:T(1024)S(1)} %add_rsqrt_fusion, f32[1024]{0:T(1024)S(1)} %divide_multiply_fusion, f32[1024]{0:T(1024)S(1)} %multiply_divide_fusion, f32[1024,1024]{1,0:T(8,128)} %copy-done, bf16[1024,1024]{0,1:T(8,128)(2,1)} %all-gather.5.cloned.1.call-done, ...), kind=kOutput, calls=%fused_computation.6 | convolution fusion | flops 2160064512 | bytes 10510336 | tf_op jit(solution)/shard_map/dot_general | solution.py:37
  217.3 1.1 broadcast_in_dim.32
  218.4 6.0 %all-to-all-start.6 = ((f32[64,1,2048]{2,1,0:T(1,128)}), f32[64,1,2048]{2,1,0:T(1,128)S(1)}, u32[]{:S(2)}, u32[]{:S(2)}) async-start(f32[64,1,2048]{2,1,0:T(1,128)} %broadcast_in_dim.32), calls=%async_computation.6 | async-start | bytes 1048576 | tf_op jit(solution)/shard_map/all_to_all | solution.py:13
  224.4 3.9 %copy.14 = bf16[1024,1024]{1,0:T(8,128)(2,1)} copy(bf16[1024,1024]{0,1:T(8,128)(2,1)} %get-tuple-element.10) | data formatting | bytes 4194304
  228.4 13.3 %all-to-all-done.6 = f32[64,1,2048]{2,1,0:T(1,128)S(1)} async-done(((f32[64,1,2048]{2,1,0:T(1,128)}), f32[64,1,2048]{2,1,0:T(1,128)S(1)}, u32[]{:S(2)}, u32[]{:S(2)}) %all-to-all-start.6) | async-done | bytes 524320 | tf_op jit(solution)/shard_map/all_to_all | solution.py:13
  241.7 0.3 reduce_sum.119
  242.0 0.6 slice_subtract_fusion
  (16 shorter events, 0.2 us)
Async XLA Ops:
  7.2 87.5 %copy-start.1 = (bf16[1024,1024]{1,0:T(8,128)(2,1)S(1)}, bf16[1024,1024]{1,0:T(8,128)(2,1)}, u32[]{:S(2)}) copy-start(bf16[1024,1024]{1,0:T(8,128)(2,1)} %param.5) | copy-start | bytes 6291460
  7.2 85.4 %all-gather.3.cloned.1.call-start = ((), (), s32[]{:S(2)}) async-start(), calls=%async_computation.7 | async-start | bytes 2129920 | tf_op jit(solution)/shard_map/all_gather | solution.py:46
  7.9 190.4 %all-gather.5.cloned.1.call-start = ((), (), s32[]{:S(2)}) async-start(), calls=%async_computation.8 | async-start | bytes 2129920 | tf_op jit(solution)/shard_map/all_gather | solution.py:47
  98.6 1.9 copy-start
  190.4 19.9 %all-to-all-start.5 = ((f32[64,1,1024]{2,1,0:T(1,128)}), f32[64,1,1024]{2,1,0:T(1,128)S(1)}, u32[]{:S(2)}, u32[]{:S(2)}) async-start(f32[64,1,1024]{2,1,0:T(1,128)} %broadcast_in_dim.31), calls=%async_computation.5 | async-start | bytes 524288 | tf_op jit(solution)/shard_map/all_to_all | solution.py:13
  218.4 23.3 %all-to-all-start.6 = ((f32[64,1,2048]{2,1,0:T(1,128)}), f32[64,1,2048]{2,1,0:T(1,128)S(1)}, u32[]{:S(2)}, u32[]{:S(2)}) async-start(f32[64,1,2048]{2,1,0:T(1,128)} %broadcast_in_dim.32), calls=%async_computation.6 | async-start | bytes 1048576 | tf_op jit(solution)/shard_map/all_to_all | solution.py:13
Sparse Core Ops, SparseCore 0:
  10.8 81.7 all-gather.2
  95.3 75.9 all-gather.4
where the time goes:
time: 250 us; the launch traced here: 249 us
  waiting for transfers between devices  106 us (42%)
  blocking collectives  59.9 us (24%)
  matrix products  39 us (16%)
  between operations  14.2 us (6%)
  starting transfers between devices  14 us (6%)
  local copies, waits for them, and re-layouts  8.12 us (3%)
  other arithmetic  7.8 us (3%)
    all_gather x1, waiting for transfers between devices, local(): lax.all_gather(view_codes, 'proto', axis=1, tiled=True)  81.8 us
    all_to_all x5, blocking collectives, copy_for_each(): return lax.all_to_all(copies, axis, split_axis=0, concat_axis=0, tiled=True)  59.9 us
    all_to_all x2, waiting for transfers between devices, copy_for_each(): return lax.all_to_all(copies, axis, split_axis=0, concat_axis=0, tiled=True)  23.2 us
    dot_general x3, matrix products, local(): col_part = jnp.dot(scale_rows, kernel, precision=lax.Precision.HIGHEST)  14.9 us
    all_to_all x2, starting transfers between devices, copy_for_each(): return lax.all_to_all(copies, axis, split_axis=0, concat_axis=0, tiled=True)  13.9 us
    dot_general x3, matrix products, local(): row_part = jnp.dot(kernel, scale_cols, precision=lax.Precision.HIGHEST)  13.3 us
    dot_general x2, matrix products, view_scores(): jnp.dot(embedded, unit_prototype_rows.T, preferred_element_type=jnp.float32)  10.9 us
    unnamed x5, local copies, waits for them, and re-layouts  5.86 us
  transfers between devices with their start and end apart: 4, of which 3 were waited for; matrix products, arithmetic and copies ran while one was open for 18% of the time, Pallas kernels for 0%

commit v1 on v0

--- a/solution.py
+++ b/solution.py
@@ -6,6 +6,12 @@
 SINK_ITERS = 3
 EPSILON = 0.05
 SOFTMAX_TEMP_VALUE = 0.1
+
+
+def tiled_gather(x, axis, dim):
+    size = lax.axis_size(axis)
+    repeats = [size if d == dim else 1 for d in range(x.ndim)]
+    return lax.all_to_all(jnp.tile(x, repeats), axis, split_axis=dim, concat_axis=dim, tiled=True)
 
 
 def copy_for_each(shard, axis):
@@ -43,7 +49,7 @@
 def local(view_codes, predictor_view_embeddings, prototypes):
     unit_prototype_rows = normalized(prototypes)
     whole_first, whole_second = (
-        lax.all_gather(view_codes, "proto", axis=1, tiled=True),
+        tiled_gather(view_codes, "proto", 1),
         lax.all_gather(predictor_view_embeddings, "proto", axis=1, tiled=True),
     )
     scores_codes = view_scores(whole_first, unit_prototype_rows)

time: 250 us -> 230 us (0.920)
  waiting for transfers between devices: 106 us -> 73.5 us
  starting transfers between devices: 14 us -> 26.6 us
    all_gather x1 -> x0, waiting for transfers between devices: 81.8 us -> none  [local(): lax.all_gather(view_codes, 'proto', axis=1, tiled=True)]
    all_to_all x0 -> x1, waiting for transfers between devices: none -> 49.6 us  [tiled_gather(): lax.all_to_all(jnp.tile(x, repeats), axis, split_axis=dim, concat_axis=di...]
    all_to_all x0 -> x1, starting transfers between devices: none -> 13.1 us  [tiled_gather(): lax.all_to_all(jnp.tile(x, repeats), axis, split_axis=dim, concat_axis=di...]
where the time goes in v1:
time: 230 us; the launch traced here: 229 us
  waiting for transfers between devices  73.5 us (32%)
  blocking collectives  59.3 us (26%)
  matrix products  39 us (17%)
  starting transfers between devices  26.6 us (12%)
  between operations  14.2 us (6%)
  local copies, waits for them, and re-layouts  10.5 us (5%)
  other arithmetic  6.21 us (3%)
    all_to_all x5, blocking collectives, copy_for_each(): return lax.all_to_all(copies, axis, split_axis=0, concat_axis=0, tiled=True)  59.3 us
    all_to_all x1, waiting for transfers between devices, tiled_gather(): lax.all_to_all(jnp.tile(x, repeats), axis, split_axis=dim, concat_axis=di...  49.6 us
    all_to_all x2, waiting for transfers between devices, copy_for_each(): return lax.all_to_all(copies, axis, split_axis=0, concat_axis=0, tiled=True)  23.2 us
    dot_general x3, matrix products, local(): col_part = jnp.dot(scale_rows, kernel, precision=lax.Precision.HIGHEST)  14.9 us
    all_to_all x2, starting transfers between devices, copy_for_each(): return lax.all_to_all(copies, axis, split_axis=0, concat_axis=0, tiled=True)  13.4 us
    dot_general x3, matrix products, local(): row_part = jnp.dot(kernel, scale_cols, precision=lax.Precision.HIGHEST)  13.3 us
    all_to_all x1, starting transfers between devices, tiled_gather(): lax.all_to_all(jnp.tile(x, repeats), axis, split_axis=dim, concat_axis=di...  13.1 us
    dot_general x2, matrix products, view_scores(): jnp.dot(embedded, unit_prototype_rows.T, preferred_element_type=jnp.float32)  10.9 us
  transfers between devices with their start and end apart: 4, of which 3 were waited for; matrix products, arithmetic and copies ran while one was open for 18% of the time, Pallas kernels for 0%

profile of v1, /device:TPU:1, one launch (start us, length us, event | category | flops | bytes accessed | tf_op | source)
XLA Modules:
  0.0 229.3 jit_solution(16280516851337928532)
XLA Ops:
  7.2 2.3 %tile.2 = bf16[1024,64,16]{0,2,1:T(8,128)(2,1)} broadcast(bf16[1024,16]{0,1:T(8,128)(2,1)} %param.3), dimensions={0,2} | broadcast | bytes 2129920 | tf_op jit(solution)/shard_map/tile | solution.py:14
  9.5 13.1 %all-to-all-start = ((bf16[1024,64,16]{0,2,1:T(8,128)(2,1)}), bf16[1024,64,16]{0,2,1:T(8,128)(2,1)S(1)}, u32[]{:S(2)}, u32[]{:S(2)}) async-start(bf16[1024,64,16]{0,2,1:T(8,128)(2,1)} %tile.2), calls=%async_computation | async-start | bytes 4194304 | tf_op jit(solution)/shard_map/all_to_all | solution.py:14
  22.7 0.0 all-gather.2.cloned.1.call-start
  22.7 0.7 all-gather.2.cloned.1.call-update
  23.4 2.1 fusion
  25.5 49.6 %all-to-all-done = bf16[1024,64,16]{0,2,1:T(8,128)(2,1)S(1)} async-done(((bf16[1024,64,16]{0,2,1:T(8,128)(2,1)}), bf16[1024,64,16]{0,2,1:T(8,128)(2,1)S(1)}, u32[]{:S(2)}, u32[]{:S(2)}) %all-to-all-start) | async-done | bytes 2097184 | tf_op jit(solution)/shard_map/all_to_all | solution.py:14
  75.1 0.5 multiply_reduce_fusion.1
  75.5 4.0 %multiply_exponential_fusion = f32[1024,1024]{1,0:T(8,128)S(1)} fusion(bf16[1024,1024]{0,1:T(8,128)(2,1)S(1)} %bitcast.46, f32[1024]{0:T(1024)S(1)} %add_rsqrt_fusion.1, bf16[1024,1024]{1,0:T(8,128)(2,1)} %param.5, f32[1024]{0:T(1024)S(1)} %add_rsqrt_fusion.2), kind=kOutput, calls=%fused_computation.25 | convolution fusion | flops 2152726528 | bytes 8396800 | tf_op jit(solution)/shard_map/dot_general | solution.py:43
  79.5 0.0 copy-start
  79.5 1.9 copy-done
  81.5 3.6 %fusion.14 = f32[1,1024]{1,0:T(1,128)S(1)} fusion(f32[1024,1024]{1,0:T(8,128)S(1)} %multiply_exponential_fusion), kind=kOutput, calls=%fused_computation.19 | convolution fusion | flops 12582912 | bytes 4198400 | tf_op jit(solution)/shard_map/dot_general | solution.py:63
  85.0 8.0 %all_to_all.51 = f32[4,1,1024]{2,1,0:T(1,128)S(1)} all-to-all(f32[4,1,1024]{2,1,0:T(1,128)S(1)} %broadcast_in_dim.26), channel_id=1, replica_groups=mesh['batch'=4,'proto'=64] {'batch'}, dimensions={0} | all-to-all | bytes 32768 | tf_op jit(solution)/shard_map/all_to_all | solution.py:19
  93.1 4.4 %fusion.12 = f32[1,1024]{1,0:T(1,128)S(1)} fusion(f32[1024,1]{0,1:T(1,128)S(1)} %bitcast.54, f32[1024,1024]{1,0:T(8,128)} %copy-done), kind=kOutput, calls=%fused_computation.17 | convolution fusion | flops 12582912 | bytes 4202496 | tf_op jit(solution)/shard_map/dot_general | solution.py:66
  97.5 0.1 broadcast_in_dim.27
  97.7 19.1 %all_to_all.52 = f32[64,1,1024]{2,1,0:T(1,128)S(1)} all-to-all(f32[64,1,1024]{2,1,0:T(1,128)S(1)} %broadcast_in_dim.27), channel_id=1, replica_groups=mesh['batch'=4,'proto'=64] {'proto'}, dimensions={0} | all-to-all | bytes 524288 | tf_op jit(solution)/shard_map/all_to_all | solution.py:19
  116.7 0.2 reduce_sum.111
  116.9 5.6 %fusion.10 = f32[1,1024]{1,0:T(1,128)S(1)} fusion(f32[1024,1]{0,1:T(1,128)S(1)} %bitcast.55, f32[1024,1024]{1,0:T(8,128)} %copy-done), kind=kOutput, calls=%fused_computation.15 | convolution fusion | flops 12582912 | bytes 4202496 | tf_op jit(solution)/shard_map/dot_general | solution.py:63
  122.6 6.6 %all_to_all.53 = f32[4,1,1024]{2,1,0:T(1,128)S(1)} all-to-all(f32[4,1,1024]{2,1,0:T(1,128)S(1)} %broadcast_in_dim.28), channel_id=1, replica_groups=mesh['batch'=4,'proto'=64] {'batch'}, dimensions={0} | all-to-all | bytes 32768 | tf_op jit(solution)/shard_map/all_to_all | solution.py:19
  129.2 4.4 %fusion.8 = f32[1,1024]{1,0:T(1,128)S(1)} fusion(f32[1024,1]{0,1:T(1,128)S(1)} %bitcast.56, f32[1024,1024]{1,0:T(8,128)} %copy-done), kind=kOutput, calls=%fused_computation.13 | convolution fusion | flops 12582912 | bytes 4202496 | tf_op jit(solution)/shard_map/dot_general | solution.py:66
  133.6 0.1 broadcast_in_dim.29
  133.8 19.0 %all_to_all.54 = f32[64,1,1024]{2,1,0:T(1,128)S(1)} all-to-all(f32[64,1,1024]{2,1,0:T(1,128)S(1)} %broadcast_in_dim.29), channel_id=1, replica_groups=mesh['batch'=4,'proto'=64] {'proto'}, dimensions={0} | all-to-all | bytes 524288 | tf_op jit(solution)/shard_map/all_to_all | solution.py:19
  152.7 0.2 reduce_sum.113
  152.9 5.6 %fusion.6 = f32[1,1024]{1,0:T(1,128)S(1)} fusion(f32[1024,1]{0,1:T(1,128)S(1)} %bitcast.57, f32[1024,1024]{1,0:T(8,128)} %copy-done), kind=kOutput, calls=%fused_computation.11 | convolution fusion | flops 12582912 | bytes 4202496 | tf_op jit(solution)/shard_map/dot_general | solution.py:63
  158.6 0.0 copy-start.1
  158.6 6.7 %all_to_all.55 = f32[4,1,1024]{2,1,0:T(1,128)S(1)} all-to-all(f32[4,1,1024]{2,1,0:T(1,128)S(1)} %broadcast_in_dim.30), channel_id=1, replica_groups=mesh['batch'=4,'proto'=64] {'batch'}, dimensions={0} | all-to-all | bytes 32768 | tf_op jit(solution)/shard_map/all_to_all | solution.py:19
  165.3 4.4 %fusion.4 = f32[1,1024]{1,0:T(1,128)S(1)} fusion(f32[1024,1]{0,1:T(1,128)S(1)} %bitcast.53, f32[1024,1024]{1,0:T(8,128)} %copy-done), kind=kOutput, calls=%fused_computation.8 | convolution fusion | flops 12582912 | bytes 4202496 | tf_op jit(solution)/shard_map/dot_general | solution.py:66
  169.8 0.8 broadcast_in_dim.31
  170.6 7.4 %all-to-all-start.6 = ((f32[64,1,1024]{2,1,0:T(1,128)}), f32[64,1,1024]{2,1,0:T(1,128)S(1)}, u32[]{:S(2)}, u32[]{:S(2)}) async-start(f32[64,1,1024]{2,1,0:T(1,128)} %broadcast_in_dim.31), calls=%async_computation.6 | async-start | bytes 524288 | tf_op jit(solution)/shard_map/all_to_all | solution.py:19
  178.0 0.0 all-gather.2.cloned.1.call-done
  178.0 2.1 multiply_reduce_fusion
  180.1 9.9 %all-to-all-done.6 = f32[64,1,1024]{2,1,0:T(1,128)S(1)} async-done(((f32[64,1,1024]{2,1,0:T(1,128)}), f32[64,1,1024]{2,1,0:T(1,128)S(1)}, u32[]{:S(2)}, u32[]{:S(2)}) %all-to-all-start.6) | async-done | bytes 262176 | tf_op jit(solution)/shard_map/all_to_all | solution.py:19
  190.0 0.2 reduce_sum.115
  190.2 0.0 copy-done.1
  190.2 6.9 %fusion.2 = (f32[1024]{0:T(1024)S(1)}, f32[1024]{0:T(1024)S(1)}, bf16[1024,1024]{0,1:T(8,128)(2,1)}) fusion(f32[1024]{0:T(1024)S(1)} %add_rsqrt_fusion, f32[1024]{0:T(1024)S(1)} %divide_multiply_fusion, f32[1024]{0:T(1024)S(1)} %multiply_divide_fusion, f32[1024,1024]{1,0:T(8,128)} %copy-done, bf16[1024,1024]{0,1:T(8,128)(2,1)} %all-gather.2.cloned.1.call-done, ...), kind=kOutput, calls=%fused_computation.6 | convolution fusion | flops 2160064512 | bytes 10510336 | tf_op jit(solution)/shard_map/dot_general | solution.py:43
  197.1 1.1 broadcast_in_dim.32
  198.2 6.0 %all-to-all-start.7 = ((f32[64,1,2048]{2,1,0:T(1,128)}), f32[64,1,2048]{2,1,0:T(1,128)S(1)}, u32[]{:S(2)}, u32[]{:S(2)}) async-start(f32[64,1,2048]{2,1,0:T(1,128)} %broadcast_in_dim.32), calls=%async_computation.7 | async-start | bytes 1048576 | tf_op jit(solution)/shard_map/all_to_all | solution.py:19
  204.2 3.9 %copy.16 = bf16[1024,1024]{1,0:T(8,128)(2,1)} copy(bf16[1024,1024]{0,1:T(8,128)(2,1)} %get-tuple-element.12) | data formatting | bytes 4194304
  208.2 13.3 %all-to-all-done.7 = f32[64,1,2048]{2,1,0:T(1,128)S(1)} async-done(((f32[64,1,2048]{2,1,0:T(1,128)}), f32[64,1,2048]{2,1,0:T(1,128)S(1)}, u32[]{:S(2)}, u32[]{:S(2)}) %all-to-all-start.7) | async-done | bytes 524320 | tf_op jit(solution)/shard_map/all_to_all | solution.py:19
  221.5 0.3 reduce_sum.119
  221.8 0.6 slice_subtract_fusion
  (16 shorter events, 0.2 us)
Async XLA Ops:
  9.5 65.5 %all-to-all-start = ((bf16[1024,64,16]{0,2,1:T(8,128)(2,1)}), bf16[1024,64,16]{0,2,1:T(8,128)(2,1)S(1)}, u32[]{:S(2)}, u32[]{:S(2)}) async-start(bf16[1024,64,16]{0,2,1:T(8,128)(2,1)} %tile.2), calls=%async_computation | async-start | bytes 4194304 | tf_op jit(solution)/shard_map/all_to_all | solution.py:14
  22.7 155.4 %all-gather.2.cloned.1.call-start = ((), (), s32[]{:S(2)}) async-start(), calls=%async_computation.8 | async-start | bytes 2129920 | tf_op jit(solution)/shard_map/all_gather | solution.py:53
  79.5 1.9 copy-start
  158.6 31.6 %copy-start.1 = (bf16[1024,1024]{1,0:T(8,128)(2,1)S(1)}, bf16[1024,1024]{1,0:T(8,128)(2,1)}, u32[]{:S(2)}) copy-start(bf16[1024,1024]{1,0:T(8,128)(2,1)} %param.5) | copy-start | bytes 6291460
  170.6 19.4 %all-to-all-start.6 = ((f32[64,1,1024]{2,1,0:T(1,128)}), f32[64,1,1024]{2,1,0:T(1,128)S(1)}, u32[]{:S(2)}, u32[]{:S(2)}) async-start(f32[64,1,1024]{2,1,0:T(1,128)} %broadcast_in_dim.31), calls=%async_computation.6 | async-start | bytes 524288 | tf_op jit(solution)/shard_map/all_to_all | solution.py:19
  198.2 23.3 %all-to-all-start.7 = ((f32[64,1,2048]{2,1,0:T(1,128)}), f32[64,1,2048]{2,1,0:T(1,128)S(1)}, u32[]{:S(2)}, u32[]{:S(2)}) async-start(f32[64,1,2048]{2,1,0:T(1,128)} %broadcast_in_dim.32), calls=%async_computation.7 | async-start | bytes 1048576 | tf_op jit(solution)/shard_map/all_to_all | solution.py:19
Sparse Core Ops, SparseCore 0:
  26.2 81.1 all-gather.1
